TPU v7x, 32 devices: a whole 2x2x4 slice. The times are simulated.
32 devices in a mesh: dp: 8 (over z, core), row: 2 (over y), col: 2 (over x).
Axes of the slice: x: 2, y: 2, z: 4, core: 2. Of those that a mesh axis runs over, the one named last changes fastest.
Arguments:
- patches: bfloat16 [4096, 1408], P(('dp', 'row', 'col')), may hold values from -6 to 6
- norm_gain: float32 [1408], replicated, may hold values from 0.5 to 1.5
- norm_bias: float32 [1408], replicated, may hold values from -3 to 3
- up_weight: bfloat16 [1408, 6144], P('col', 'row'), may hold values from -0.15625 to 0.15625
- up_bias: float32 [6144], P('row'), may hold values from -3 to 3
- down_weight: bfloat16 [6144, 1408], P('row', 'col'), may hold values from -0.078125 to 0.078125
- down_bias: float32 [1408], replicated, may hold values from -3 to 3
- cotangent: bfloat16 [4096, 1408], P(('dp', 'row', 'col')), may hold values from -6 to 6
Outputs:
- output: float32 [4096, 1408], P(('dp', 'row', 'col'))
- patch_grad: float32 [4096, 1408], P(('dp', 'row', 'col'))
- up_grad: float32 [1408, 6144], P('col', 'row')
- down_grad: float32 [6144, 1408], P('row', 'col')
- bias_grad: float32 [6144], P('row')
- norm_grad: float32 [2, 1408], replicated
All inputs are finite; a program needn't handle non-finite values.
Results may differ from a plain program's by a relative error of at most 0.0055.
Values may be sent and summed in bfloat16 or wider, within the bound.
A program may use at most 128 MiB of HBM per device.

v0:
```python
import math
import jax
import jax.numpy as jnp
from jax import lax
from jax.sharding import PartitionSpec as P

EPSILON = 1e-06
GELU_ROOT = 0.7978845608028654
GELU_CUBIC = 0.044715


def gelu_value(value):
    inner = jnp.tanh(GELU_ROOT * (value + GELU_CUBIC * value * value * value))
    return 0.5 * value * (1.0 + inner)


def gelu_slope(value):
    inner = jnp.tanh(GELU_ROOT * (value + GELU_CUBIC * value * value * value))
    return 0.5 * (1.0 + inner) + 0.5 * value * (1.0 - inner * inner) * GELU_ROOT * (
        1.0 + 3.0 * GELU_CUBIC * value * value
    )


def contract_rows(left, right):
    return lax.dot_general(
        left, right, (((0,), (0,)), ((), ())), preferred_element_type=jnp.float32
    )


def contract_cols(left, right):
    return lax.dot_general(
        left, right, (((1,), (1,)), ((), ())), preferred_element_type=jnp.float32
    )


def on_device(patches, norm_gain, norm_bias, up_weight, up_bias, down_weight, down_bias, cotangent):
    n_row = lax.axis_size("row")
    n_col = lax.axis_size("col")
    n_replica = lax.axis_size("dp")
    local_rows = patches.shape[0]
    width = patches.shape[1]
    half_width = width // n_col
    group_rows = n_row * local_rows
    scaling = 1.0 / math.sqrt(local_rows * n_row * n_col * n_replica)
    wide_patches = patches.astype(jnp.float32)
    centred = wide_patches - jnp.mean(wide_patches, axis=1, keepdims=True)
    inverse_spread = lax.rsqrt(jnp.mean(centred * centred, axis=1, keepdims=True) + EPSILON)
    standard = centred * inverse_spread
    normed = (standard * norm_gain + norm_bias).astype(jnp.bfloat16)
    swapped = lax.all_to_all(normed, "col", split_axis=1, concat_axis=0, tiled=True)
    swapped = swapped.reshape(n_col, local_rows, half_width)
    gathered = lax.all_gather(swapped, "row", axis=1, tiled=True)
    normed_all = gathered.reshape(n_col * group_rows, half_width)
    preact = (
        lax.psum_scatter(
            jnp.dot(normed_all, up_weight, preferred_element_type=jnp.float32),
            "col",
            scatter_dimension=0,
            tiled=True,
        )
        + up_bias
    )
    activated = gelu_value(preact).astype(jnp.bfloat16)
    down_full = lax.all_gather(down_weight, "col", axis=1, tiled=True)
    projected = lax.psum_scatter(
        jnp.dot(activated, down_full, preferred_element_type=jnp.float32),
        "row",
        scatter_dimension=0,
        tiled=True,
    )
    output = projected + down_bias + wide_patches
    upstream = lax.all_gather(cotangent, "row", axis=0, tiled=True)
    down_partial = contract_rows(activated, upstream)
    down_grad = lax.psum_scatter(down_partial, "col", scatter_dimension=1, tiled=True)
    slope = (contract_cols(upstream, down_full) * gelu_slope(preact)).astype(jnp.bfloat16)
    slope_all = lax.all_gather(slope, "col", axis=0, tiled=True)
    up_grad = contract_rows(normed_all, slope_all)
    bias_grad = jnp.sum(slope_all.astype(jnp.float32), axis=0)
    up_grad, bias_grad, down_grad = lax.psum((up_grad, bias_grad, down_grad), "dp")
    partial_back = contract_cols(slope_all, up_weight).reshape(n_col, n_row, local_rows, half_width)
    summed_back = lax.psum_scatter(partial_back, "row", scatter_dimension=1, tiled=True)
    summed_back = summed_back.reshape(n_col, local_rows, half_width)
    normed_back = lax.all_to_all(summed_back, "col", split_axis=0, concat_axis=2, tiled=True)
    normed_back = normed_back.reshape(local_rows, width)
    norm_terms = jnp.stack([jnp.sum(normed_back * standard, axis=0), jnp.sum(normed_back, axis=0)])
    norm_grad = lax.psum(norm_terms, ("dp", "row", "col"))
    scaled = normed_back * norm_gain
    back = inverse_spread * (
        scaled
        - jnp.mean(scaled, axis=1, keepdims=True)
        - standard * jnp.mean(scaled * standard, axis=1, keepdims=True)
    )
    patch_grad = back + cotangent.astype(jnp.float32)
    return (
        output,
        patch_grad,
        up_grad * scaling,
        down_grad * scaling,
        bias_grad * scaling,
        norm_grad * scaling,
    )


def solution(mesh):
    in_specs = (
        P(("dp", "row", "col"), None),
        P(),
        P(),
        P("col", "row"),
        P("row"),
        P("row", "col"),
        P(),
        P(("dp", "row", "col"), None),
    )
    out_specs = (
        P(("dp", "row", "col"), None),
        P(("dp", "row", "col"), None),
        P("col", "row"),
        P("row", "col"),
        P("row"),
        P(),
    )
    return jax.shard_map(
        on_device, mesh=mesh, in_specs=in_specs, out_specs=out_specs, check_vma=False
    )
```

profile of v0, /device:TPU:0, one launch (start us, length us, event | category | flops | bytes accessed | tf_op | source)
XLA Modules:
  0.0 874.7 jit_solution(3099713600413117997)
XLA Ops:
  9.1 10.3 %all_to_all.31 = bf16[128,2,704]{0,2,1:T(8,128)(2,1)S(1)} all-to-all(bf16[128,2,704]{0,2,1:T(8,128)(2,1)S(1)} %bitcast.30), channel_id=1, replica_groups=mesh['dp'=8,'row'=2,'col'=2] {'col'}, dimensions={1} | all-to-all | bytes 720896 | tf_op jit(solution)/shard_map/all_to_all | solution.py:50
  19.3 9.7 %all_gather.12 = bf16[2,256,704]{1,2,0:T(8,128)(2,1)S(1)} all-gather(bf16[2,128,704]{1,2,0:T(8,128)(2,1)S(1)} %bitcast.31), channel_id=1, replica_groups=mesh['dp'=8,'row'=2,'col'=2] {'row'}, dimensions={1}, use_global_device_ids=true | all-gather | bytes 1081344 | tf_op jit(solution)/shard_map/all_gather | solution.py:52
  30.0 7.2 fusion.23
  38.2 9.0 %all_gather.14 = bf16[256,1408]{1,0:T(8,128)(2,1)} all-gather(bf16[128,1408]{1,0:T(8,128)(2,1)S(1)} %copy-done.5), channel_id=1, replica_groups=mesh['dp'=8,'row'=2,'col'=2] {'row'}, dimensions={0}, use_global_device_ids=true | all-gather | bytes 1081344 | tf_op jit(solution)/shard_map/all_gather | solution.py:72
  47.1 74.6 %all-gather.3.cloned.1.call-done = bf16[3072,1408]{0,1:T(8,128)(2,1)} async-done(((bf16[3072,704]{0,1:T(8,128)(2,1)}), bf16[3072,1408]{0,1:T(8,128)(2,1)}) %all-gather.3.cloned.1.call-update) | async-done | bytes 8650768 | tf_op jit(solution)/shard_map/all_gather | solution.py:64
  121.7 80.0 %reduce-scatter.5.cloned.1.call-done = f32[256,3072]{1,0:T(8,128)} async-done(((f32[512,3072]{1,0:T(8,128)}), f32[256,3072]{1,0:T(8,128)}) %reduce-scatter.5.cloned.1.call-update) | async-done | bytes 3145744 | tf_op jit(solution)/shard_map/reduce_scatter | solution.py:55
  201.7 9.9 %fusion = bf16[256,3072]{1,0:T(8,128)(2,1)} fusion(bf16[256,1408]{1,0:T(8,128)(2,1)} %all_gather.14, bf16[3072,1408]{0,1:T(8,128)(2,1)} %all-gather.3.cloned.1.call-done, f32[256,3072]{1,0:T(8,128)} %reduce-scatter.5.cloned.1.call-done, f32[3072]{0:T(1024)S(1)} %copy-done.8), kind=kOutput, calls=%fused_computation.6 | convolution fusion | flops 2230321152 | bytes 14102528 | tf_op jit(solution)/shard_map/dot_general | solution.py:31
  211.7 10.9 %fusion.21 = f32[3072,1408]{0,1:T(8,128)} fusion(bf16[256,1408]{1,0:T(8,128)(2,1)} %all_gather.14, f32[256,3072]{1,0:T(8,128)S(1)} %copy-done.2, f32[3072]{0:T(1024)S(1)} %copy-done.8), kind=kOutput, calls=%fused_computation.40 | convolution fusion | flops 2222456832 | bytes 21180416 | tf_op jit(solution)/shard_map/dot_general | solution.py:25
  222.9 33.8 %all-gather.5.cloned.1.call-done = bf16[512,3072]{1,0:T(8,128)(2,1)} async-done(((bf16[256,3072]{1,0:T(8,128)(2,1)}), bf16[512,3072]{1,0:T(8,128)(2,1)}) %all-gather.5.cloned.1.call-update) | async-done | bytes 3145744 | tf_op jit(solution)/shard_map/all_gather | solution.py:76
  256.7 5.6 fusion.24
  262.3 0.9 reshape.62
  263.3 1.2 copy.17
  264.6 9.0 %fusion.22 = f32[256,1408]{1,0:T(8,128)} fusion(bf16[3072,1408]{0,1:T(8,128)(2,1)} %all-gather.3.cloned.1.call-done, f32[256,3072]{1,0:T(8,128)} %reduce-scatter.5.cloned.1.call-done, f32[3072]{0:T(1024)S(1)} %copy-done.8), kind=kOutput, calls=%fused_computation.41 | convolution fusion | flops 2222456832 | bytes 13250560 | tf_op jit(solution)/shard_map/dot_general | solution.py:66
  273.6 8.0 fusion.25
  281.7 172.1 %reduce-scatter.11.cloned.1.call-done = f32[3072,704]{0,1:T(8,128)} async-done(((f32[3072,1408]{0,1:T(8,128)}), f32[3072,704]{0,1:T(8,128)}) %reduce-scatter.11.cloned.1.call-update) | async-done | bytes 8650768 | tf_op jit(solution)/shard_map/reduce_scatter | solution.py:74
  453.9 27.3 %reduce-scatter.9.cloned.1.call-done = f32[2,1,128,704]{2,3,0,1:T(8,128)} async-done(((f32[2,2,128,704]{2,3,0,1:T(8,128)}), f32[2,1,128,704]{2,3,0,1:T(8,128)}) %reduce-scatter.9.cloned.1.call-update) | async-done | bytes 720912 | tf_op jit(solution)/shard_map/reduce_scatter | solution.py:81
  481.2 3.5 all-to-all-start.1
  484.7 2.6 convert_reduce_fusion
  487.3 28.4 %psum.30 = f32[3072]{0:T(1024)S(1)} all-reduce(f32[3072]{0:T(1024)S(1)} %convert_reduce_fusion), channel_id=1, replica_groups=mesh['dp'=8,'row'=2,'col'=2] {'dp'}, use_global_device_ids=true, to_apply=%region_11.0 | all-reduce | flops 3072 | bytes 24576 | tf_op jit(solution)/shard_map/psum | solution.py:79
  517.5 38.8 %psum.31 = f32[2,1408]{1,0:T(2,128)S(1)} all-reduce(f32[2,1408]{1,0:T(2,128)S(1)} %pad_maximum_fusion), channel_id=1, replica_groups=mesh['dp'=8,'row'=2,'col'=2] {'dp','row','col'}, use_global_device_ids=true, to_apply=%region_14.0 | all-reduce | flops 2816 | bytes 22528 | tf_op jit(solution)/shard_map/psum | solution.py:86
  556.9 2.5 fusion.17
  559.4 295.5 %all-reduce.3.cloned.1.call-done = (f32[704,3072]{1,0:T(8,128)}, f32[3072,704]{0,1:T(8,128)}) async-done(((f32[704,3072]{1,0:T(8,128)}, f32[3072,704]{0,1:T(8,128)}), (f32[704,3072]{1,0:T(8,128)}, f32[3072,704]{0,1:T(8,128)})) %all-reduce.3.cloned.1.call-update) | async-done | bytes 17301520 | tf_op jit(solution)/shard_map/psum | solution.py:79
  855.0 8.6 broadcast_multiply_fusion.1
  863.5 4.3 broadcast_multiply_fusion
  (55 shorter events, 6.7 us)
Async XLA Ops:
  7.2 1.0 copy-start
  7.2 1.4 copy-start.7
  7.2 1.4 copy-start.9
  7.2 114.5 %all-gather.3.cloned.1.call-start = ((), (), s32[]{:S(2)}) async-start(), calls=%async_computation.7 | async-start | bytes 12976128 | tf_op jit(solution)/shard_map/all_gather | solution.py:64
  7.9 193.8 %reduce-scatter.5.cloned.1.call-start = ((), (), s32[]{:S(2)}) async-start(), calls=%async_computation.6 | async-start | bytes 9437184 | tf_op jit(solution)/shard_map/reduce_scatter | solution.py:55
  29.1 0.9 copy-start.3
  37.2 1.0 copy-start.5
  37.2 164.5 %copy-start.8 = (f32[3072]{0:T(1024)S(1)}, f32[3072]{0:T(1024)}, u32[]{:S(2)}) copy-start(f32[3072]{0:T(1024)} %param.12) | copy-start | bytes 36868
  37.2 219.5 %all-gather.5.cloned.1.call-start = ((), (), s32[]{:S(2)}) async-start(), calls=%async_computation.9 | async-start | bytes 4718592 | tf_op jit(solution)/shard_map/all_gather | solution.py:76
  201.7 10.0 %copy-start.2 = (f32[256,3072]{1,0:T(8,128)S(1)}, f32[256,3072]{1,0:T(8,128)}, u32[]{:S(2)}) copy-start(f32[256,3072]{1,0:T(8,128)} %reduce-scatter.5.cloned.1.call-done) | copy-start | bytes 9437188
  211.7 242.1 %reduce-scatter.11.cloned.1.call-start = ((), (), s32[]{:S(2)}) async-start(), calls=%async_computation.11 | async-start | bytes 25952256 | tf_op jit(solution)/shard_map/reduce_scatter | solution.py:74
  222.7 258.5 %reduce-scatter.9.cloned.1.call-start = ((), (), s32[]{:S(2)}) async-start(), calls=%async_computation.10 | async-start | bytes 2162688 | tf_op jit(solution)/shard_map/reduce_scatter | solution.py:81
  264.5 9.1 %copy-start.4 = (bf16[2,88,8,256]{3,2,0,1:T(8,128)(2,1)S(1)}, bf16[2,88,8,256]{3,2,0,1:T(8,128)(2,1)}, u32[]{:S(2)}) copy-start(bf16[2,88,8,256]{3,2,0,1:T(8,128)(2,1)} %copy-done.3) | copy-start | bytes 2162692
  264.5 292.4 %reduce-scatter.7.cloned.1.call-start = ((), (), s32[]{:S(2)}) async-start(), calls=%async_computation.8 | async-start | bytes 2162688 | tf_op jit(solution)/shard_map/reduce_scatter | solution.py:65
  273.6 581.4 %all-reduce.3.cloned.1.call-start = ((), (), s32[]{:S(2)}) async-start(), calls=%async_computation.12 | async-start | bytes 34603008 | tf_op jit(solution)/shard_map/psum | solution.py:79
  481.2 35.1 %all-to-all-start.1 = ((f32[2,128,704]{1,2,0:T(8,128)}), f32[2,128,704]{1,2,0:T(8,128)S(1)}, u32[]{:S(2)}, u32[]{:S(2)}) async-start(f32[2,128,704]{1,2,0:T(8,128)} %bitcast.32), calls=%async_computation.4 | async-start | bytes 1441792 | tf_op jit(solution)/shard_map/all_to_all | solution.py:83
  484.7 72.2 %copy-start.6 = (bf16[128,1408]{1,0:T(8,128)(2,1)S(1)}, bf16[128,1408]{1,0:T(8,128)(2,1)}, u32[]{:S(2)}) copy-start(bf16[128,1408]{1,0:T(8,128)(2,1)} %param.15) | copy-start | bytes 1081348
  484.7 72.2 %copy-start.10 = (f32[1408]{0:T(1024)S(1)}, f32[1408]{0:T(1024)}, u32[]{:S(2)}) copy-start(f32[1408]{0:T(1024)} %param.14) | copy-start | bytes 16900
  855.0 8.6 copy-start.1
Sparse Core Ops, SparseCore 0:
  9.6 112.0 all-gather.2
  124.5 77.1 reduce-scatter.4
  211.8 44.8 all-gather.4
  258.9 194.8 reduce-scatter.10
  456.4 24.6 reduce-scatter.8
  483.3 24.6 reduce-scatter.6
  511.2 343.7 all-reduce.2
where the time goes:
time: 875 us
  waiting for transfers between devices  684 us (78%)
  blocking collectives  96.1 us (11%)
  matrix products  50.6 us (6%)
  other arithmetic  20.7 us (2%)
  between operations  14.3 us (2%)
    psum x1, waiting for transfers between devices, on_device(): lax.psum((up_grad, bias_grad, down_grad), 'dp')  296 us
    reduce_scatter x1, waiting for transfers between devices, on_device(): lax.psum_scatter(down_partial, 'col', scatter_dimension=1, tiled=True)  172 us
    reduce_scatter x1, waiting for transfers between devices, on_device(): lax.psum_scatter(jnp.dot(normed_all, up_weight, preferred_element_type=jn...  80 us
    all_gather x1, waiting for transfers between devices, on_device(): down_full = lax.all_gather(down_weight, 'col', axis=1, tiled=True)  74.6 us
    psum x1, blocking collectives, on_device(): norm_grad = lax.psum(norm_terms, ('dp', 'row', 'col'))  38.8 us
    all_gather x1, waiting for transfers between devices, on_device(): slope_all = lax.all_gather(slope, 'col', axis=0, tiled=True)  33.8 us
    psum x1, blocking collectives, on_device(): lax.psum((up_grad, bias_grad, down_grad), 'dp')  28.4 us
    reduce_scatter x1, waiting for transfers between devices, on_device(): lax.psum_scatter(partial_back, 'row', scatter_dimension=1, tiled=True)  27.3 us
  transfers between devices with their start and end apart: 8, of which 6 were waited for; matrix products, arithmetic and copies ran while one was open for 6% of the time, Pallas kernels for 0%

commit v1 on v0

--- a/solution.py
+++ b/solution.py
@@ -7,6 +7,12 @@
 EPSILON = 1e-06
 GELU_ROOT = 0.7978845608028654
 GELU_CUBIC = 0.044715
+
+
+def gather_pair(x, name, dim):
+    other = lax.ppermute(x, name, [(0, 1), (1, 0)])
+    row_of_blocks = jnp.concatenate([x, other], axis=dim)
+    return jnp.roll(row_of_blocks, lax.axis_index(name) * x.shape[dim], axis=dim)
 
 
 def gelu_value(value):
@@ -61,7 +67,7 @@
         + up_bias
     )
     activated = gelu_value(preact).astype(jnp.bfloat16)
-    down_full = lax.all_gather(down_weight, "col", axis=1, tiled=True)
+    down_full = gather_pair(down_weight, "col", 1)
     projected = lax.psum_scatter(
         jnp.dot(activated, down_full, preferred_element_type=jnp.float32),
         "row",

time: 875 us -> 892 us (1.019)
  other arithmetic: 20.7 us -> 41.4 us
    ppermute x0 -> x1, waiting for transfers between devices: none -> 151 us  [gather_pair(): other = lax.ppermute(x, name, [(0, 1), (1, 0)])]
    reduce_scatter x1, waiting for transfers between devices: 80 us -> 0.01 us  [on_device(): lax.psum_scatter(jnp.dot(normed_all, up_weight, preferred_element_type=jn...]
    all_gather x1 -> x0, waiting for transfers between devices: 74.6 us -> none  [on_device(): down_full = lax.all_gather(down_weight, 'col', axis=1, tiled=True)]
    concatenate x0 -> x1, other arithmetic: none -> 17.8 us  [gather_pair(): jnp.roll(row_of_blocks, lax.axis_index(name) * x.shape[dim], axis=dim)]
  transfers between devices with their start and end apart: 8 -> 8, of which waited for: 6 -> 5; matrix products, arithmetic and copies ran while one was open for 6% -> 7% of each run, Pallas kernels for 0% -> 0%
where the time goes in v1:
time: 892 us; the launch traced here: 891 us
  waiting for transfers between devices  681 us (76%)
  blocking collectives  95.9 us (11%)
  matrix products  50 us (6%)
  other arithmetic  41.4 us (5%)
  between operations  14.2 us (2%)
    psum x1, waiting for transfers between devices, on_device(): lax.psum((up_grad, bias_grad, down_grad), 'dp')  296 us
    reduce_scatter x1, waiting for transfers between devices, on_device(): lax.psum_scatter(down_partial, 'col', scatter_dimension=1, tiled=True)  172 us
    ppermute x1, waiting for transfers between devices, gather_pair(): other = lax.ppermute(x, name, [(0, 1), (1, 0)])  151 us
    psum x1, blocking collectives, on_device(): norm_grad = lax.psum(norm_terms, ('dp', 'row', 'col'))  38.6 us
    all_gather x1, waiting for transfers between devices, on_device(): slope_all = lax.all_gather(slope, 'col', axis=0, tiled=True)  34.9 us
    psum x1, blocking collectives, on_device(): lax.psum((up_grad, bias_grad, down_grad), 'dp')  28.4 us
    reduce_scatter x1, waiting for transfers between devices, on_device(): lax.psum_scatter(partial_back, 'row', scatter_dimension=1, tiled=True)  26.6 us
    dot_general x2, matrix products, contract_rows(): lax.dot_general(left, right, (((0,), (0,)), ((), ())), preferred_element_...  18.7 us
  transfers between devices with their start and end apart: 8, of which 5 were waited for; matrix products, arithmetic and copies ran while one was open for 7% of the time, Pallas kernels for 0%

profile of v1, /device:TPU:0, one launch (start us, length us, event | category | flops | bytes accessed | tf_op | source)
XLA Modules:
  0.0 891.4 jit_solution(7184788667319267889)
XLA Ops:
  8.3 1.2 fusion.23
  9.6 1.3 fusion.17
  11.1 10.3 %all_to_all.31 = bf16[128,2,704]{0,2,1:T(8,128)(2,1)S(1)} all-to-all(bf16[128,2,704]{0,2,1:T(8,128)(2,1)S(1)} %bitcast.36), channel_id=1, replica_groups=mesh['dp'=8,'row'=2,'col'=2] {'col'}, dimensions={1} | all-to-all | bytes 720896 | tf_op jit(solution)/shard_map/all_to_all | solution.py:56
  21.4 9.7 %all_gather.9 = bf16[2,256,704]{1,2,0:T(8,128)(2,1)S(1)} all-gather(bf16[2,128,704]{1,2,0:T(8,128)(2,1)S(1)} %bitcast.37), channel_id=1, replica_groups=mesh['dp'=8,'row'=2,'col'=2] {'row'}, dimensions={1}, use_global_device_ids=true | all-gather | bytes 1081344 | tf_op jit(solution)/shard_map/all_gather | solution.py:58
  32.0 6.8 fusion.27
  39.7 8.9 %all_gather.10 = bf16[256,1408]{1,0:T(8,128)(2,1)} all-gather(bf16[128,1408]{1,0:T(8,128)(2,1)S(1)} %copy-done.5), channel_id=1, replica_groups=mesh['dp'=8,'row'=2,'col'=2] {'row'}, dimensions={0}, use_global_device_ids=true | all-gather | bytes 1081344 | tf_op jit(solution)/shard_map/all_gather | solution.py:78
  48.7 151.1 %collective-permute-done = bf16[3072,704]{0,1:T(8,128)(2,1)} collective-permute-done((bf16[3072,704]{0,1:T(8,128)(2,1)}, bf16[3072,704]{0,1:T(8,128)(2,1)}, u32[]{:S(2)}, u32[]{:S(2)}) %collective-permute-start) | collective-permute-done | bytes 4325408 | tf_op jit(solution)/shard_map/ppermute | solution.py:13
  199.8 17.8 %fusion.2 = bf16[3072,1408]{0,1:T(8,128)(2,1)} fusion(s32[]{:T(128)S(6)} %select_n.14, bf16[3072,704]{0,1:T(8,128)(2,1)} %param.13, bf16[3072,704]{0,1:T(8,128)(2,1)} %collective-permute-done), kind=kLoop, calls=%fused_computation.6 | loop fusion | flops 34603008 | bytes 17301508 | tf_op jit(solution)/shard_map/jit(_roll_dynamic)/concatenate | solution.py:15
  217.6 9.9 %fusion.4 = bf16[256,3072]{1,0:T(8,128)(2,1)} fusion(bf16[256,1408]{1,0:T(8,128)(2,1)} %all_gather.10, bf16[3072,1408]{0,1:T(8,128)(2,1)} %fusion.2, f32[256,3072]{1,0:T(8,128)} %reduce-scatter.5.cloned.1.call-done, f32[3072]{0:T(1024)S(1)} %copy-done.7), kind=kOutput, calls=%fused_computation.14 | convolution fusion | flops 2230321152 | bytes 14102528 | tf_op jit(solution)/shard_map/dot_general | solution.py:37
  227.7 10.7 %fusion.25 = f32[3072,1408]{0,1:T(8,128)} fusion(bf16[256,1408]{1,0:T(8,128)(2,1)} %all_gather.10, f32[256,3072]{1,0:T(8,128)S(1)} %copy-done.2, f32[3072]{0:T(1024)S(1)} %copy-done.7), kind=kOutput, calls=%fused_computation.48 | convolution fusion | flops 2222456832 | bytes 21180416 | tf_op jit(solution)/shard_map/dot_general | solution.py:31
  238.5 34.9 %all-gather.2.cloned.1.call-done = bf16[512,3072]{1,0:T(8,128)(2,1)} async-done(((bf16[256,3072]{1,0:T(8,128)(2,1)}), bf16[512,3072]{1,0:T(8,128)(2,1)}) %all-gather.2.cloned.1.call-update) | async-done | bytes 3145744 | tf_op jit(solution)/shard_map/all_gather | solution.py:82
  273.4 5.6 fusion.28
  281.3 9.0 %fusion.26 = f32[256,1408]{1,0:T(8,128)} fusion(bf16[3072,1408]{0,1:T(8,128)(2,1)} %fusion.2, f32[256,3072]{1,0:T(8,128)} %reduce-scatter.5.cloned.1.call-done, f32[3072]{0:T(1024)S(1)} %copy-done.7), kind=kOutput, calls=%fused_computation.49 | convolution fusion | flops 2222456832 | bytes 13250560 | tf_op jit(solution)/shard_map/dot_general | solution.py:72
  290.3 8.0 fusion.29
  298.4 172.2 %reduce-scatter.11.cloned.1.call-done = f32[3072,704]{0,1:T(8,128)} async-done(((f32[3072,1408]{0,1:T(8,128)}), f32[3072,704]{0,1:T(8,128)}) %reduce-scatter.11.cloned.1.call-update) | async-done | bytes 8650768 | tf_op jit(solution)/shard_map/reduce_scatter | solution.py:80
  471.4 26.6 %reduce-scatter.9.cloned.1.call-done = f32[2,1,128,704]{2,3,0,1:T(8,128)} async-done(((f32[2,2,128,704]{2,3,0,1:T(8,128)}), f32[2,1,128,704]{2,3,0,1:T(8,128)}) %reduce-scatter.9.cloned.1.call-update) | async-done | bytes 720912 | tf_op jit(solution)/shard_map/reduce_scatter | solution.py:87
  498.0 3.7 all-to-all-start.1
  501.7 2.5 convert_reduce_fusion
  504.2 28.4 %psum.30 = f32[3072]{0:T(1024)S(1)} all-reduce(f32[3072]{0:T(1024)S(1)} %convert_reduce_fusion), channel_id=1, replica_groups=mesh['dp'=8,'row'=2,'col'=2] {'dp'}, use_global_device_ids=true, to_apply=%region_11.12 | all-reduce | flops 3072 | bytes 24576 | tf_op jit(solution)/shard_map/psum | solution.py:85
  534.4 38.6 %psum.31 = f32[2,1408]{1,0:T(2,128)S(1)} all-reduce(f32[2,1408]{1,0:T(2,128)S(1)} %pad_maximum_fusion), channel_id=1, replica_groups=mesh['dp'=8,'row'=2,'col'=2] {'dp','row','col'}, use_global_device_ids=true, to_apply=%region_14.15 | all-reduce | flops 2816 | bytes 22528 | tf_op jit(solution)/shard_map/psum | solution.py:92
  573.6 2.5 fusion.21
  576.1 295.5 %all-reduce.3.cloned.1.call-done = (f32[704,3072]{1,0:T(8,128)}, f32[3072,704]{0,1:T(8,128)}) async-done(((f32[704,3072]{1,0:T(8,128)}, f32[3072,704]{0,1:T(8,128)}), (f32[704,3072]{1,0:T(8,128)}, f32[3072,704]{0,1:T(8,128)})) %all-reduce.3.cloned.1.call-update) | async-done | bytes 17301520 | tf_op jit(solution)/shard_map/psum | solution.py:85
  871.7 8.6 broadcast_multiply_fusion.1
  880.2 4.3 broadcast_multiply_fusion
  (51 shorter events, 9.0 us)
Async XLA Ops:
  7.2 210.4 %reduce-scatter.5.cloned.1.call-start = ((), (), s32[]{:S(2)}) async-start(), calls=%async_computation.6 | async-start | bytes 9437184 | tf_op jit(solution)/shard_map/reduce_scatter | solution.py:61
  31.1 0.9 copy-start.3
  38.8 1.0 copy-start.5
  38.8 234.6 %all-gather.2.cloned.1.call-start = ((), (), s32[]{:S(2)}) async-start(), calls=%async_computation.8 | async-start | bytes 4718592 | tf_op jit(solution)/shard_map/all_gather | solution.py:82
  38.8 160.9 %collective-permute-start = (bf16[3072,704]{0,1:T(8,128)(2,1)}, bf16[3072,704]{0,1:T(8,128)(2,1)}, u32[]{:S(2)}, u32[]{:S(2)}) collective-permute-start(bf16[3072,704]{0,1:T(8,128)(2,1)} %param.13), channel_id=1, source_target_pairs={{0,1},{1,0},{2,3},{3,2},{4,5},{5,4},{6,7},{7,6},{8,9},{9,8},{10,11... | collective-permute-start | bytes 12976136 | tf_op jit(solution)/shard_map/ppermute | solution.py:13
  48.7 168.8 %copy-start.7 = (f32[3072]{0:T(1024)S(1)}, f32[3072]{0:T(1024)}, u32[]{:S(2)}) copy-start(f32[3072]{0:T(1024)} %param.12) | copy-start | bytes 36868
  217.5 10.2 %copy-start.2 = (f32[256,3072]{1,0:T(8,128)S(1)}, f32[256,3072]{1,0:T(8,128)}, u32[]{:S(2)}) copy-start(f32[256,3072]{1,0:T(8,128)} %reduce-scatter.5.cloned.1.call-done) | copy-start | bytes 9437188
  227.5 243.1 %reduce-scatter.11.cloned.1.call-start = ((), (), s32[]{:S(2)}) async-start(), calls=%async_computation.10 | async-start | bytes 25952256 | tf_op jit(solution)/shard_map/reduce_scatter | solution.py:80
  238.5 259.6 %reduce-scatter.9.cloned.1.call-start = ((), (), s32[]{:S(2)}) async-start(), calls=%async_computation.9 | async-start | bytes 2162688 | tf_op jit(solution)/shard_map/reduce_scatter | solution.py:87
  281.2 9.1 %copy-start.4 = (bf16[2,88,8,256]{3,2,0,1:T(8,128)(2,1)S(1)}, bf16[2,88,8,256]{3,2,0,1:T(8,128)(2,1)}, u32[]{:S(2)}) copy-start(bf16[2,88,8,256]{3,2,0,1:T(8,128)(2,1)} %copy-done.3) | copy-start | bytes 2162692
  281.2 292.4 %reduce-scatter.7.cloned.1.call-start = ((), (), s32[]{:S(2)}) async-start(), calls=%async_computation.7 | async-start | bytes 2162688 | tf_op jit(solution)/shard_map/reduce_scatter | solution.py:71
  290.3 581.4 %all-reduce.3.cloned.1.call-start = ((), (), s32[]{:S(2)}) async-start(), calls=%async_computation.11 | async-start | bytes 34603008 | tf_op jit(solution)/shard_map/psum | solution.py:85
  470.6 0.7 copy-start.6
  498.0 36.0 %copy-start = (bf16[128,1408]{1,0:T(8,128)(2,1)S(1)}, bf16[128,1408]{1,0:T(8,128)(2,1)}, u32[]{:S(2)}) copy-start(bf16[128,1408]{1,0:T(8,128)(2,1)} %param.8) | copy-start | bytes 1081348
  498.0 35.2 %all-to-all-start.1 = ((f32[2,128,704]{1,2,0:T(8,128)}), f32[2,128,704]{1,2,0:T(8,128)S(1)}, u32[]{:S(2)}, u32[]{:S(2)}) async-start(f32[2,128,704]{1,2,0:T(8,128)} %bitcast.38), calls=%async_computation.4 | async-start | bytes 1441792 | tf_op jit(solution)/shard_map/all_to_all | solution.py:89
  501.7 71.9 %copy-start.8 = (f32[1408]{0:T(1024)S(1)}, f32[1408]{0:T(1024)}, u32[]{:S(2)}) copy-start(f32[1408]{0:T(1024)} %param.14) | copy-start | bytes 16900
  871.7 8.6 copy-start.1
Sparse Core Ops, SparseCore 0:
  38.9 145.1 reduce-scatter.4
  227.6 45.7 all-gather.1
  275.7 194.8 reduce-scatter.10
  473.3 24.6 reduce-scatter.8
  500.1 24.7 reduce-scatter.6
  527.9 343.6 all-reduce.2
